TPU v7x, 32 devices: a whole 2x2x4 slice. The times are simulated.
32 devices in a mesh: seq: 8 (over z, y), head: 4 (over x, core).
Axes of the slice: x: 2, y: 2, z: 4, core: 2. Of those that a mesh axis runs over, the one named last changes fastest.
Arguments:
- queries: bfloat16 [4096, 8192], P(('seq', 'head')), may hold values from -8 to 8
- keys: bfloat16 [4096, 1024], P(('seq', 'head')), may hold values from -8 to 8
- values: bfloat16 [4096, 1024], P(('seq', 'head')), may hold values from -6 to 6
- selected: int32 [32, 8], P('seq'), may hold values from 0 to 31, as said below
- counts: int32 [32], P('seq'), may hold values from 1 to 8
- block_slot: int32 [32], P('seq'), may hold values from 0 to 31, as said below
Outputs:
- attended: bfloat16 [4096, 8192], P(('seq', 'head'))
Inputs may be any that keep to these rules, and one draw needn't show every extreme that they name: A permutation of 0 to 31. Block b's rows of keys and values start at row 128 * block_slot[b]; its owner shard is block_slot[b] // 4. The 4 blocks of one sequence shard (blocks s * 4 onward) have distinct owner shards, and block_slot[b] % 4 == b % 4. `selected`: row q lists its live entries first: entry 0 is q itself, the other live entries are distinct blocks of earlier sequence shards; entries from counts[q] on are 0. Over the live entries of the 4 rows of one sequence shard, at most 2 distinct blocks have the same owner shard, and in every draw some shard reaches 2 from some owner.
All inputs are finite; a program needn't handle non-finite values.
Results may differ from a plain program's by a relative error of at most 0.0049.
Values may be sent and summed in bfloat16 or wider, within the bound.
A program may use at most 128 MiB of HBM per device.

v0:
```python
import math

import jax
import jax.numpy as jnp
from jax import lax
from jax.sharding import PartitionSpec as P

QUERY_HEADS = 64
KEY_VALUE_HEADS = 8
HEAD_SIZE = 128
BLOCK_ROWS = 128
SELECTION_COUNT = 8
CAP = 2


def body(queries, keys, values, selected, counts, block_slot):
    seq_count = lax.axis_size("seq")
    my_shard = lax.axis_index("seq")
    blk_seq = selected.shape[0]
    block_count = blk_seq * seq_count
    highest = lax.Precision.HIGHEST
    q_heads, k_heads, v_heads = (
        lax.all_to_all(queries, "head", split_axis=1, concat_axis=0, tiled=True),
        lax.all_to_all(keys, "head", split_axis=1, concat_axis=0, tiled=True),
        lax.all_to_all(values, "head", split_axis=1, concat_axis=0, tiled=True),
    )
    kv_width = k_heads.shape[1]
    kv_heads_dev = kv_width // HEAD_SIZE
    all_slots = lax.all_gather(block_slot, "seq", axis=0, tiled=True)
    block_ids = jnp.arange(block_count, dtype=jnp.int32)
    slot_hit = (all_slots[:, None] == block_ids[None, :]).astype(jnp.float32)
    entry_range = jnp.arange(SELECTION_COUNT, dtype=jnp.int32)
    entry_live = (entry_range[None, :] < counts[:, None]).astype(jnp.float32)
    entry_hit = (selected.reshape(-1)[:, None] == block_ids[None, :]).astype(jnp.float32)
    wanted_blocks = jnp.max(entry_hit * entry_live.reshape(-1, 1), axis=0)
    wanted_slots = jnp.dot(wanted_blocks, slot_hit, precision=highest)
    wanted_grid = wanted_slots.reshape(seq_count, blk_seq)
    rank_grid = jnp.cumsum(wanted_grid, axis=1) - wanted_grid
    owner_base = (jnp.arange(seq_count, dtype=jnp.int32) * CAP).astype(jnp.float32)
    place_slot = (owner_base[:, None] + rank_grid).reshape(-1)
    place_block = jnp.dot(slot_hit, place_slot, precision=highest)
    place_entry = jnp.dot(entry_hit, place_block, precision=highest).astype(jnp.int32)
    place_entry = jnp.clip(place_entry, 0, seq_count * CAP - 1).reshape(blk_seq, SELECTION_COUNT)
    wanted_by = lax.all_to_all(
        wanted_grid.astype(jnp.int32), "seq", split_axis=0, concat_axis=0, tiled=True
    )
    wanted_float = wanted_by.astype(jnp.float32)
    send_rank = jnp.cumsum(wanted_float, axis=1) - wanted_float
    cap_range = jnp.arange(CAP, dtype=jnp.float32)
    pick_map = wanted_float[:, None, :] * (
        send_rank[:, None, :] == cap_range[None, :, None]
    ).astype(jnp.float32)
    pick_map = pick_map.reshape(seq_count * CAP, blk_seq)
    source_tile = jnp.sum(
        pick_map * jnp.arange(blk_seq, dtype=jnp.float32)[None, :], axis=1
    ).astype(jnp.int32)
    is_valid = jnp.sum(pick_map, axis=1) > 0.5
    own_keys = k_heads.reshape(blk_seq, BLOCK_ROWS, kv_width)
    own_values = v_heads.reshape(blk_seq, BLOCK_ROWS, kv_width)
    send_keys = jnp.where(
        is_valid[:, None, None], own_keys[source_tile], jnp.zeros((), jnp.bfloat16)
    )
    send_values = jnp.where(
        is_valid[:, None, None], own_values[source_tile], jnp.zeros((), jnp.bfloat16)
    )
    got_keys, got_values = (
        lax.all_to_all(send_keys, "seq", split_axis=0, concat_axis=0, tiled=True),
        lax.all_to_all(send_values, "seq", split_axis=0, concat_axis=0, tiled=True),
    )
    heads_per_group = QUERY_HEADS // KEY_VALUE_HEADS
    score_scale = 1.0 / math.sqrt(HEAD_SIZE)
    query_block_list = q_heads.reshape(
        blk_seq, BLOCK_ROWS, kv_heads_dev, heads_per_group, HEAD_SIZE
    )
    got_keys = got_keys.reshape(seq_count * CAP, BLOCK_ROWS, kv_heads_dev, HEAD_SIZE)
    got_values = got_values.reshape(seq_count * CAP, BLOCK_ROWS, kv_heads_dev, HEAD_SIZE)
    row_range = jnp.arange(BLOCK_ROWS, dtype=jnp.int32)

    def attend(operands):
        local_block, query_tile, place_row, chosen, live_count = operands
        key_block_rows = got_keys[place_row].reshape(
            SELECTION_COUNT * BLOCK_ROWS, kv_heads_dev, HEAD_SIZE
        )
        value_block_rows = got_values[place_row].reshape(
            SELECTION_COUNT * BLOCK_ROWS, kv_heads_dev, HEAD_SIZE
        )
        scores = (
            jnp.einsum(
                "igmd,kgd->gmik", query_tile, key_block_rows, preferred_element_type=jnp.float32
            )
            * score_scale
        )
        query_pos = (my_shard * blk_seq + local_block) * BLOCK_ROWS + row_range
        key_pos = (chosen[:, None] * BLOCK_ROWS + row_range[None, :]).reshape(-1)
        live_entry = jnp.repeat(entry_range < live_count, BLOCK_ROWS)
        visible = live_entry[None, :] & (key_pos[None, :] <= query_pos[:, None])
        scores = jnp.where(visible[None, None], scores, -jnp.inf)
        row_top = jnp.max(scores, axis=-1, keepdims=True)
        weights = jnp.exp(scores - row_top)
        probability = (weights / jnp.sum(weights, axis=-1, keepdims=True)).astype(jnp.bfloat16)
        mixed_out = jnp.einsum(
            "gmik,kgd->igmd", probability, value_block_rows, preferred_element_type=jnp.float32
        )
        return mixed_out.astype(jnp.bfloat16).reshape(
            BLOCK_ROWS, kv_heads_dev * heads_per_group * HEAD_SIZE
        )

    attended = lax.map(
        attend,
        (jnp.arange(blk_seq, dtype=jnp.int32), query_block_list, place_entry, selected, counts),
    )
    attended = attended.reshape(blk_seq * BLOCK_ROWS, kv_heads_dev * heads_per_group * HEAD_SIZE)
    return lax.all_to_all(attended, "head", split_axis=0, concat_axis=1, tiled=True)


def solution(mesh):
    return jax.shard_map(
        body,
        mesh=mesh,
        in_specs=(
            P(("seq", "head"), None),
            P(("seq", "head"), None),
            P(("seq", "head"), None),
            P("seq", None),
            P("seq"),
            P("seq"),
        ),
        out_specs=P(("seq", "head"), None),
        check_vma=False,
    )
```

profile of v0, /device:TPU:0, one launch (start us, length us, event | category | flops | bytes accessed | tf_op | source)
XLA Modules:
  0.0 245.5 jit_solution(9089203433233708243)
XLA Ops:
  2.8 13.1 %all-reduce = s32[32]{0:T(128)S(1)} all-reduce(s32[32]{0:T(128)S(1)} %dynamic-update-slice), channel_id=1, replica_groups=mesh['seq'=8,'head'=4] {'seq'}, use_global_device_ids=true, to_apply=%add | all-reduce | flops 32 | bytes 256
  18.7 3.3 %all-to-all-start = ((s32[8,1,4]{2,1,0:T(1,128)}), s32[8,1,4]{2,1,0:T(1,128)S(1)}, u32[]{:S(2)}, u32[]{:S(2)}) async-start(s32[8,1,4]{2,1,0:T(1,128)} %copy.56), calls=%async_computation | async-start | bytes 8192 | tf_op jit(solution)/shard_map/all_to_all | solution.py:44
  26.0 2.5 %all-to-all-done = s32[8,1,4]{2,1,0:T(1,128)S(1)} async-done(((s32[8,1,4]{2,1,0:T(1,128)}), s32[8,1,4]{2,1,0:T(1,128)S(1)}, u32[]{:S(2)}, u32[]{:S(2)}) %all-to-all-start) | async-done | bytes 160 | tf_op jit(solution)/shard_map/all_to_all | solution.py:44
  28.4 3.4 %all-to-all-start.1 = ((bf16[128,4,256]{2,0,1:T(8,128)(2,1)}), bf16[128,4,256]{2,0,1:T(8,128)(2,1)S(1)}, u32[]{:S(2)}, u32[]{:S(2)}) async-start(bf16[128,4,256]{2,0,1:T(8,128)(2,1)} %copy.61), calls=%async_computation.1 | async-start | bytes 524288 | tf_op jit(solution)/shard_map/all_to_all | solution.py:25
  33.6 4.2 %all-to-all-done.1 = bf16[128,4,256]{2,0,1:T(8,128)(2,1)S(1)} async-done(((bf16[128,4,256]{2,0,1:T(8,128)(2,1)}), bf16[128,4,256]{2,0,1:T(8,128)(2,1)S(1)}, u32[]{:S(2)}, u32[]{:S(2)}) %all-to-all-start.1) | async-done | bytes 262176 | tf_op jit(solution)/shard_map/all_to_all | solution.py:25
  37.8 3.4 %all-to-all-start.3 = ((bf16[128,4,256]{2,0,1:T(8,128)(2,1)}), bf16[128,4,256]{2,0,1:T(8,128)(2,1)S(1)}, u32[]{:S(2)}, u32[]{:S(2)}) async-start(bf16[128,4,256]{2,0,1:T(8,128)(2,1)} %copy.64), calls=%async_computation.3 | async-start | bytes 524288 | tf_op jit(solution)/shard_map/all_to_all | solution.py:24
  42.1 5.1 %all-to-all-done.3 = bf16[128,4,256]{2,0,1:T(8,128)(2,1)S(1)} async-done(((bf16[128,4,256]{2,0,1:T(8,128)(2,1)}), bf16[128,4,256]{2,0,1:T(8,128)(2,1)S(1)}, u32[]{:S(2)}, u32[]{:S(2)}) %all-to-all-start.3) | async-done | bytes 262176 | tf_op jit(solution)/shard_map/all_to_all | solution.py:24
  49.0 28.7 %all_to_all.83 = bf16[16,128,256]{2,1,0:T(8,128)(2,1)S(1)} all-to-all(bf16[16,128,256]{2,1,0:T(8,128)(2,1)S(1)} %get-tuple-element.263), channel_id=1, replica_groups=mesh['seq'=8,'head'=4] {'seq'}, dimensions={0} | all-to-all | bytes 2097152 | tf_op jit(solution)/shard_map/all_to_all | solution.py:68
  77.8 3.6 %all-to-all-start.4 = ((bf16[16,128,256]{2,1,0:T(8,128)(2,1)}), bf16[16,128,256]{2,1,0:T(8,128)(2,1)S(1)}, u32[]{:S(2)}, u32[]{:S(2)}) async-start(bf16[16,128,256]{2,1,0:T(8,128)(2,1)} %get-tuple-element.262), calls=%async_computation.4 | async-start | bytes 2097152 | tf_op jit(solution)/shard_map/all_to_all | solution.py:67
  81.3 4.1 %copy.65 = bf16[128,8192]{0,1:T(8,128)(2,1)} copy(bf16[128,8192]{1,0:T(8,128)(2,1)} %param.8) | data formatting | bytes 4194304 | tf_op args[0]
  85.4 21.4 %all-to-all-done.4 = bf16[16,128,256]{2,1,0:T(8,128)(2,1)S(1)} async-done(((bf16[16,128,256]{2,1,0:T(8,128)(2,1)}), bf16[16,128,256]{2,1,0:T(8,128)(2,1)S(1)}, u32[]{:S(2)}, u32[]{:S(2)}) %all-to-all-start.4) | async-done | bytes 1048608 | tf_op jit(solution)/shard_map/all_to_all | solution.py:67
  106.9 4.6 %all-to-all-start.5 = ((bf16[128,4,2048]{0,2,1:T(8,128)(2,1)}), bf16[128,4,2048]{0,2,1:T(8,128)(2,1)}, u32[]{:S(2)}, u32[]{:S(2)}) async-start(bf16[128,4,2048]{0,2,1:T(8,128)(2,1)} %bitcast.14), calls=%async_computation.5 | async-start | bytes 4194304 | tf_op jit(solution)/shard_map/all_to_all | solution.py:23
  112.8 24.4 %all-to-all-done.5 = bf16[128,4,2048]{0,2,1:T(8,128)(2,1)} async-done(((bf16[128,4,2048]{0,2,1:T(8,128)(2,1)}), bf16[128,4,2048]{0,2,1:T(8,128)(2,1)}, u32[]{:S(2)}, u32[]{:S(2)}) %all-to-all-start.5) | async-done | bytes 2097184 | tf_op jit(solution)/shard_map/all_to_all | solution.py:23
  137.2 76.2 %while.14 = (s32[]{:T(128)}, bf16[4,128,2048]{1,2,0:T(8,128)(2,1)}, s32[4,8]{1,0:T(4,128)S(1)}, bf16[16,128,2,128]{3,2,1,0:T(2,128)(2,1)S(1)}, s32[4]{0:T(128)S(...) while((s32[]{:T(128)}, bf16[4,128,2048]{1,2,0:T(8,128)(2,1)}, ...), condition=%wide.region_8.9_spmd.clone.clone, body=%wide.region_5.8_spmd.clone.clone.sunk | while | flops 1086852352 | bytes 22315460 | solution.py:108
  141.2 1.6 gather_fusion
  142.8 6.8 %fusion.77 = (f32[2,8,128]{2,1,0:T(8,128)S(1)}, f32[2,8,128,1024]{2,3,1,0:T(8,128)}) fusion(pred[128,1024]{0,1:T(8,128)(4,1)S(1)} %compare_and_fusion.2, bf16[1024,2,128,1]{2,1,0,3:T(2,128)(2,1)S(1)} %bitcast.113, bf16[4,128,2,8,128]{1,4,3,2,0:T(8,128)(2,1)} %get-tuple-element.362, s32[]{:T(128)} %get-tuple-element.341), kind=kOutput, calls=%fused_computation.75.clone.1 | convolution fusion | flops 545260544 | bytes 9576960 | tf_op jit(solution)/shard_map/while/body/eval_jaxpr/sub | solution.py:99
  149.6 1.6 gather_fusion.1
  151.2 4.2 %fusion.78 = bf16[2,128,8,128]{3,1,2,0:T(8,128)(2,1)S(1)} fusion(f32[2,8,128,1024]{2,3,1,0:T(8,128)} %get-tuple-element.327, f32[2,8,128]{2,1,0:T(8,128)S(1)} %get-tuple-element.328, bf16[1024,2,128,1]{2,1,0,3:T(2,128)(2,1)S(1)} %bitcast.114), kind=kOutput, calls=%fused_computation.15.clone.1 | convolution fusion | flops 541327360 | bytes 9445376 | tf_op jit(solution)/shard_map/while/body/eval_jaxpr/gmik,kgd->igmd/dot_general | solution.py:101
  160.2 1.6 gather_fusion
  161.8 6.8 %fusion.77 = (f32[2,8,128]{2,1,0:T(8,128)S(1)}, f32[2,8,128,1024]{2,3,1,0:T(8,128)}) fusion(pred[128,1024]{0,1:T(8,128)(4,1)S(1)} %compare_and_fusion.2, bf16[1024,2,128,1]{2,1,0,3:T(2,128)(2,1)S(1)} %bitcast.113, bf16[4,128,2,8,128]{1,4,3,2,0:T(8,128)(2,1)} %get-tuple-element.362, s32[]{:T(128)} %get-tuple-element.341), kind=kOutput, calls=%fused_computation.75.clone.1 | convolution fusion | flops 545260544 | bytes 9576960 | tf_op jit(solution)/shard_map/while/body/eval_jaxpr/sub | solution.py:99
  168.7 1.6 gather_fusion.1
  170.3 4.2 %fusion.78 = bf16[2,128,8,128]{3,1,2,0:T(8,128)(2,1)S(1)} fusion(f32[2,8,128,1024]{2,3,1,0:T(8,128)} %get-tuple-element.327, f32[2,8,128]{2,1,0:T(8,128)S(1)} %get-tuple-element.328, bf16[1024,2,128,1]{2,1,0,3:T(2,128)(2,1)S(1)} %bitcast.114), kind=kOutput, calls=%fused_computation.15.clone.1 | convolution fusion | flops 541327360 | bytes 9445376 | tf_op jit(solution)/shard_map/while/body/eval_jaxpr/gmik,kgd->igmd/dot_general | solution.py:101
  179.3 1.6 gather_fusion
  180.9 6.8 %fusion.77 = (f32[2,8,128]{2,1,0:T(8,128)S(1)}, f32[2,8,128,1024]{2,3,1,0:T(8,128)}) fusion(pred[128,1024]{0,1:T(8,128)(4,1)S(1)} %compare_and_fusion.2, bf16[1024,2,128,1]{2,1,0,3:T(2,128)(2,1)S(1)} %bitcast.113, bf16[4,128,2,8,128]{1,4,3,2,0:T(8,128)(2,1)} %get-tuple-element.362, s32[]{:T(128)} %get-tuple-element.341), kind=kOutput, calls=%fused_computation.75.clone.1 | convolution fusion | flops 545260544 | bytes 9576960 | tf_op jit(solution)/shard_map/while/body/eval_jaxpr/sub | solution.py:99
  187.7 1.6 gather_fusion.1
  189.3 4.2 %fusion.78 = bf16[2,128,8,128]{3,1,2,0:T(8,128)(2,1)S(1)} fusion(f32[2,8,128,1024]{2,3,1,0:T(8,128)} %get-tuple-element.327, f32[2,8,128]{2,1,0:T(8,128)S(1)} %get-tuple-element.328, bf16[1024,2,128,1]{2,1,0,3:T(2,128)(2,1)S(1)} %bitcast.114), kind=kOutput, calls=%fused_computation.15.clone.1 | convolution fusion | flops 541327360 | bytes 9445376 | tf_op jit(solution)/shard_map/while/body/eval_jaxpr/gmik,kgd->igmd/dot_general | solution.py:101
  198.3 1.6 gather_fusion
  199.9 6.8 %fusion.77 = (f32[2,8,128]{2,1,0:T(8,128)S(1)}, f32[2,8,128,1024]{2,3,1,0:T(8,128)}) fusion(pred[128,1024]{0,1:T(8,128)(4,1)S(1)} %compare_and_fusion.2, bf16[1024,2,128,1]{2,1,0,3:T(2,128)(2,1)S(1)} %bitcast.113, bf16[4,128,2,8,128]{1,4,3,2,0:T(8,128)(2,1)} %get-tuple-element.362, s32[]{:T(128)} %get-tuple-element.341), kind=kOutput, calls=%fused_computation.75.clone.1 | convolution fusion | flops 545260544 | bytes 9576960 | tf_op jit(solution)/shard_map/while/body/eval_jaxpr/sub | solution.py:99
  206.8 1.6 gather_fusion.1
  208.4 4.2 %fusion.78 = bf16[2,128,8,128]{3,1,2,0:T(8,128)(2,1)S(1)} fusion(f32[2,8,128,1024]{2,3,1,0:T(8,128)} %get-tuple-element.327, f32[2,8,128]{2,1,0:T(8,128)S(1)} %get-tuple-element.328, bf16[1024,2,128,1]{2,1,0,3:T(2,128)(2,1)S(1)} %bitcast.114), kind=kOutput, calls=%fused_computation.15.clone.1 | convolution fusion | flops 541327360 | bytes 9445376 | tf_op jit(solution)/shard_map/while/body/eval_jaxpr/gmik,kgd->igmd/dot_general | solution.py:101
  213.4 29.2 %all_to_all.84 = bf16[4,128,2048]{1,2,0:T(8,128)(2,1)S(1)} all-to-all(bf16[4,128,2048]{1,2,0:T(8,128)(2,1)} %get-tuple-element.146), channel_id=1, replica_groups=mesh['seq'=8,'head'=4] {'head'}, dimensions={0} | all-to-all | bytes 4194304 | tf_op jit(solution)/shard_map/all_to_all | solution.py:113
  242.6 2.9 %copy.72 = bf16[128,8192]{1,0:T(8,128)(2,1)} copy(bf16[128,8192]{0,1:T(8,128)(2,1)S(1)} %bitcast.115) | data formatting | bytes 4194304 | tf_op jit(solution)/shard_map/all_to_all | solution.py:113
  (91 shorter events, 30.7 us)
Async XLA Ops:
  18.7 9.8 %all-to-all-start = ((s32[8,1,4]{2,1,0:T(1,128)}), s32[8,1,4]{2,1,0:T(1,128)S(1)}, u32[]{:S(2)}, u32[]{:S(2)}) async-start(s32[8,1,4]{2,1,0:T(1,128)} %copy.56), calls=%async_computation | async-start | bytes 8192 | tf_op jit(solution)/shard_map/all_to_all | solution.py:44
  28.4 9.4 %all-to-all-start.1 = ((bf16[128,4,256]{2,0,1:T(8,128)(2,1)}), bf16[128,4,256]{2,0,1:T(8,128)(2,1)S(1)}, u32[]{:S(2)}, u32[]{:S(2)}) async-start(bf16[128,4,256]{2,0,1:T(8,128)(2,1)} %copy.61), calls=%async_computation.1 | async-start | bytes 524288 | tf_op jit(solution)/shard_map/all_to_all | solution.py:25
  37.8 9.4 %all-to-all-start.3 = ((bf16[128,4,256]{2,0,1:T(8,128)(2,1)}), bf16[128,4,256]{2,0,1:T(8,128)(2,1)S(1)}, u32[]{:S(2)}, u32[]{:S(2)}) async-start(bf16[128,4,256]{2,0,1:T(8,128)(2,1)} %copy.64), calls=%async_computation.3 | async-start | bytes 524288 | tf_op jit(solution)/shard_map/all_to_all | solution.py:24
  77.8 29.1 %all-to-all-start.4 = ((bf16[16,128,256]{2,1,0:T(8,128)(2,1)}), bf16[16,128,256]{2,1,0:T(8,128)(2,1)S(1)}, u32[]{:S(2)}, u32[]{:S(2)}) async-start(bf16[16,128,256]{2,1,0:T(8,128)(2,1)} %get-tuple-element.262), calls=%async_computation.4 | async-start | bytes 2097152 | tf_op jit(solution)/shard_map/all_to_all | solution.py:67
  106.9 30.4 %copy-start = (s32[4]{0:T(128)S(1)}, s32[4]{0:T(128)}, u32[]{:S(2)}) copy-start(s32[4]{0:T(128)} %param.12) | copy-start | bytes 52
  106.9 30.4 %all-to-all-start.5 = ((bf16[128,4,2048]{0,2,1:T(8,128)(2,1)}), bf16[128,4,2048]{0,2,1:T(8,128)(2,1)}, u32[]{:S(2)}, u32[]{:S(2)}) async-start(bf16[128,4,2048]{0,2,1:T(8,128)(2,1)} %bitcast.14), calls=%async_computation.5 | async-start | bytes 4194304 | tf_op jit(solution)/shard_map/all_to_all | solution.py:23
where the time goes:
time: 247 us; the launch traced here: 246 us
  blocking collectives  71.1 us (29%)
  waiting for transfers between devices  57.7 us (23%)
  matrix products  44.9 us (18%)
  local copies, waits for them, and re-layouts  39 us (16%)
  starting transfers between devices  18.3 us (7%)
  other arithmetic  10.8 us (4%)
  loops' own time  3.02 us (1%)
    all_to_all x1, blocking collectives, body(): lax.all_to_all(attended, 'head', split_axis=0, concat_axis=1, tiled=True)  29.2 us
    all_to_all x1, blocking collectives, body(): lax.all_to_all(send_values, 'seq', split_axis=0, concat_axis=0, tiled=True)  28.7 us
    sub x4, matrix products, attend(): weights = jnp.exp(scores - row_top)  27.4 us
    all_to_all x1, waiting for transfers between devices, body(): lax.all_to_all(queries, 'head', split_axis=1, concat_axis=0, tiled=True)  24.4 us
    all_to_all x1, waiting for transfers between devices, body(): lax.all_to_all(send_keys, 'seq', split_axis=0, concat_axis=0, tiled=True)  21.4 us
    dot_general x4, matrix products, attend(): jnp.einsum('gmik,kgd->igmd', probability, value_block_rows, preferred_ele...  16.8 us
    unnamed x1, blocking collectives  13.1 us
    unnamed x7, local copies, waits for them, and re-layouts  8.44 us
  transfers between devices with their start and end apart: 5, of which 5 were waited for; matrix products, arithmetic and copies ran while one was open for 5% of the time, Pallas kernels for 0%

commit v1 on v0

v1 whole, which is shorter than its diff:
```python
import functools
import math

import jax
import jax.numpy as jnp
from jax import lax
from jax.experimental import pallas as pl
from jax.experimental.pallas import tpu as pltpu
from jax.sharding import PartitionSpec as P

QUERY_HEADS = 64
KEY_VALUE_HEADS = 8
HEAD_SIZE = 128
BLOCK_ROWS = 128
MESH = pl.DeviceIdType.MESH


def kernel(ns, nh, groups, entries, q_ref, k_ref, v_ref, sel_ref, cnt_ref, slot_ref, out_ref,
           qbuf, obuf, kcat, vcat, diag, slots_v, slots_s,
           hs, hr, qs, qr, us, ur, ds_, dr, ys, yr, os_, or_, ss, sr, slot_sem, *kv):
    s = lax.axis_index("seq")
    h = lax.axis_index("head")
    ysz = 2 if ns % 2 == 0 else 1
    zsz = ns // ysz
    z = s // ysz
    y = s % ysz
    y_peer = s + 1 - 2 * y
    width = qbuf.shape[3]
    heads_per_group = width // HEAD_SIZE
    rotation = [nh // 2] + [d for d in range(nh - 1, 0, -1) if d != nh // 2]

    def remote(src, dst, send, recv, dev):
        return pltpu.make_async_remote_copy(
            src_ref=src, dst_ref=dst, send_sem=send, recv_sem=recv,
            device_id=dev, device_id_type=MESH)

    barrier = pltpu.get_barrier_semaphore()
    for d in range(1, nh):
        pl.semaphore_signal(barrier, inc=1, device_id=(s, (h + d) % nh), device_id_type=MESH)
    for d in range(1, ns):
        pl.semaphore_signal(barrier, inc=1, device_id=((s + d) % ns, h), device_id_type=MESH)
    pl.semaphore_wait(barrier, nh - 1 + ns - 1)

    def lanes(unit, size):
        return pl.ds(pl.multiple_of(unit * size, size), size)

    def kv_head(g, t, d):
        peer = (h + d) % nh
        src = (k_ref, v_ref)[t]
        return remote(src.at[:, lanes(peer * groups + g, HEAD_SIZE)], kv[g].at[s * nh + h, t],
                      hs.at[g, t, d - 1], hr.at[g, t, d - 1], (s, peer))

    def kv_head_in(g, t, d):
        peer = (h + nh - d) % nh
        src = (k_ref, v_ref)[t]
        return remote(src.at[:, lanes(peer * groups + g, HEAD_SIZE)], kv[g].at[s * nh + peer, t],
                      hs.at[g, t, d - 1], hr.at[g, t, d - 1], (s, peer))

    def q_head(g, d):
        peer = (h + d) % nh
        return remote(q_ref.at[:, lanes(peer * groups + g, width)], qbuf.at[g, h],
                      qs.at[g, d - 1], qr.at[g, d - 1], (s, peer))

    def q_head_in(g, d):
        peer = (h + nh - d) % nh
        return remote(q_ref.at[:, lanes(peer * groups + g, width)], qbuf.at[g, peer],
                      qs.at[g, d - 1], qr.at[g, d - 1], (s, peer))

    def slot_out(d):
        return remote(slot_ref, slots_v.at[s], ss.at[d - 1], sr.at[d - 1], ((s + d) % ns, h))

    def slot_in(d):
        peer = (s + ns - d) % ns
        return remote(slot_ref, slots_v.at[peer], ss.at[d - 1], sr.at[d - 1], (peer, h))

    for g in range(groups):
        for d in rotation:
            for t in range(2):
                kv_head(g, t, d).start()
    for d in range(1, ns):
        slot_out(d).start()
    for g in range(groups):
        for d in rotation:
            q_head(g, d).start()

    for g in range(groups):
        kv[g][s * nh + h, 0] = k_ref[:, lanes(h * groups + g, HEAD_SIZE)]
        kv[g][s * nh + h, 1] = v_ref[:, lanes(h * groups + g, HEAD_SIZE)]
        qbuf[g, h] = q_ref[:, lanes(h * groups + g, width)]
    slots_v[s] = slot_ref[...]
    pair_rows = 2 * BLOCK_ROWS
    row = lax.rem(lax.broadcasted_iota(jnp.int32, (pair_rows, BLOCK_ROWS), 0), BLOCK_ROWS)
    col = lax.broadcasted_iota(jnp.int32, (pair_rows, BLOCK_ROWS), 1)
    diag[...] = jnp.where(col <= row, 0.0, -jnp.inf).astype(jnp.float32)
    vcat[:, HEAD_SIZE:] = jnp.ones((entries * BLOCK_ROWS, HEAD_SIZE), jnp.bfloat16)

    def chunk(g, shard):
        return kv[g].at[pl.ds(shard * nh, nh)]

    def up(g, t, shard, dev):
        return remote(chunk(g, shard), chunk(g, shard), us.at[g, t], ur.at[g, t], (dev, h))

    def down(g, t, shard, dev):
        return remote(chunk(g, shard), chunk(g, shard), ds_.at[g, t], dr.at[g, t], (dev, h))

    def across(g, i, shard):
        return remote(chunk(g, shard), chunk(g, shard), ys.at[g, i], yr.at[g, i], (y_peer, h))

    def gather_start(g):
        for d in rotation:
            for t in range(2):
                kv_head_in(g, t, d).wait_recv()
        if ysz > 1:
            across(g, 0, s).start()
        if zsz > 1:
            @pl.when(z < zsz - 1)
            def _():
                up(g, 0, s, s + ysz).start()

            @pl.when(z > 0)
            def _():
                down(g, 0, s, s - ysz).start()

    def gather_step(g, t):
        below = s - (1 + t) * ysz
        above = s + (1 + t) * ysz

        @pl.when(z - 1 - t >= 0)
        def _():
            up(g, t, below, s).wait_recv()
            if t + 1 < zsz - 1:
                @pl.when(z < zsz - 1)
                def _():
                    up(g, t + 1, below, s + ysz).start()
            if ysz > 1:
                across(g, 1 + t, below).start()

        @pl.when(z + 1 + t <= zsz - 1)
        def _():
            down(g, t, above, s).wait_recv()
            if t + 1 < zsz - 1:
                @pl.when(z > 0)
                def _():
                    down(g, t + 1, above, s - ysz).start()
            if ysz > 1:
                across(g, zsz + t, above).start()

    def gather_end(g):
        if ysz > 1:
            across(g, 0, y_peer).wait_recv()
            for t in range(zsz - 1):
                @pl.when(z - 1 - t >= 0)
                def _():
                    across(g, 1 + t, y_peer - (1 + t) * ysz).wait_recv()

                @pl.when(z + 1 + t <= zsz - 1)
                def _():
                    across(g, zsz + t, y_peer + (1 + t) * ysz).wait_recv()

    def gather_drain(g):
        if ysz > 1:
            across(g, 0, s).wait_send()
        for t in range(zsz - 1):
            @pl.when((z < zsz - 1) & (z - t >= 0))
            def _():
                up(g, t, s - t * ysz, s + ysz).wait_send()

            @pl.when((z > 0) & (z + t <= zsz - 1))
            def _():
                down(g, t, s + t * ysz, s - ysz).wait_send()
            if ysz > 1:
                @pl.when(z - 1 - t >= 0)
                def _():
                    across(g, 1 + t, s - (1 + t) * ysz).wait_send()

                @pl.when(z + 1 + t <= zsz - 1)
                def _():
                    across(g, zsz + t, s + (1 + t) * ysz).wait_send()

    factor = math.log2(math.e) / math.sqrt(HEAD_SIZE)
    blk_seq = sel_ref.shape[0]

    def fetch(g, j):
        for e in range(entries):
            b = sel_ref[j, e]
            place = slots_s[lax.div(b, blk_seq), 0, lax.rem(b, blk_seq)]
            rows = slice(e * BLOCK_ROWS, (e + 1) * BLOCK_ROWS)
            kcat[rows, :] = kv[g][place, 0]
            vcat[rows, :HEAD_SIZE] = kv[g][place, 1]

    def attend(g, j):
        rest = lax.broadcasted_iota(jnp.int32, (1, (entries - 1) * BLOCK_ROWS), 1) + BLOCK_ROWS
        bias = jnp.where(rest < cnt_ref[j] * BLOCK_ROWS, 0.0, -jnp.inf).astype(jnp.float32)

        def pair(i, _):
            cols = pl.multiple_of(i * 2 * HEAD_SIZE, 2 * HEAD_SIZE)
            q2 = qbuf[g, j, :, pl.ds(cols, 2 * HEAD_SIZE)]
            q2 = jnp.concatenate([q2[:, :HEAD_SIZE], q2[:, HEAD_SIZE:]], axis=0)
            scores = lax.dot_general(q2, kcat[...], (((1,), (1,)), ((), ())),
                                     preferred_element_type=jnp.float32)
            own = scores[:, :BLOCK_ROWS] + diag[...]
            others = scores[:, BLOCK_ROWS:] + bias
            scores = jnp.concatenate([own, others], axis=1)
            top = jnp.max(scores, axis=1, keepdims=True)
            weights = jnp.exp2((scores - top) * factor).astype(jnp.bfloat16)
            mixed = jnp.dot(weights, vcat[...], preferred_element_type=jnp.float32)
            result = (mixed[:, :HEAD_SIZE] / mixed[:, HEAD_SIZE:]).astype(jnp.bfloat16)
            obuf[g, j, :, pl.ds(cols, HEAD_SIZE)] = result[:BLOCK_ROWS]
            obuf[g, j, :, pl.ds(cols + HEAD_SIZE, HEAD_SIZE)] = result[BLOCK_ROWS:]
            return 0

        lax.fori_loop(0, heads_per_group // 2, pair, 0)

    def result_out(g, d):
        peer = (h + d) % nh
        return remote(obuf.at[g, peer], out_ref.at[:, lanes(h * groups + g, width)],
                      os_.at[g, d - 1], or_.at[g, d - 1], (s, peer))

    def result_in(g, d):
        peer = (h + nh - d) % nh
        return remote(obuf.at[g, peer], out_ref.at[:, lanes(peer * groups + g, width)],
                      os_.at[g, d - 1], or_.at[g, d - 1], (s, peer))

    gather_start(0)
    for t in range(zsz - 1):
        gather_step(0, t)
    for d in range(1, ns):
        slot_in(d).wait_recv()
    slot_copy = pltpu.make_async_copy(slots_v, slots_s, slot_sem)
    slot_copy.start()
    slot_copy.wait()

    order = rotation + [0]
    pending = None
    for g in range(groups):
        steps = []
        if g + 1 < groups:
            gather_start(g + 1)
            steps = list(range(zsz - 1))
            if steps:
                gather_step(g + 1, steps.pop(0))
        gather_end(g)
        for d in order:
            j = (h + d) % nh
            fetch(g, j)
            if pending is not None:
                result_out(*pending).start()
                pending = None
            if d:
                q_head_in(g, nh - d).wait_recv()
            attend(g, j)
            if d:
                pending = (g, d)
            else:
                out_ref[:, lanes(h * groups + g, width)] = obuf[g, h]
            if steps:
                gather_step(g + 1, steps.pop(0))
        for t in steps:
            gather_step(g + 1, t)

    for g in range(groups):
        gather_drain(g)
        for d in rotation:
            for t in range(2):
                kv_head(g, t, d).wait_send()
            q_head(g, d).wait_send()
    for d in range(1, ns):
        slot_out(d).wait_send()
    for g in range(groups):
        for d in rotation:
            result_out(g, d).wait_send()
            result_in(g, d).wait_recv()


def body(queries, keys, values, selected, counts, block_slot):
    ns = lax.axis_size("seq")
    nh = lax.axis_size("head")
    blk_seq, entries = selected.shape
    rows = queries.shape[0]
    groups = keys.shape[1] // HEAD_SIZE // nh
    width = queries.shape[1] // nh // groups
    assert rows == BLOCK_ROWS and blk_seq == nh
    slots = jnp.pad(block_slot, (0, 128 - blk_seq)).reshape(1, 128)
    vmem = pl.BlockSpec(memory_space=pltpu.VMEM)
    smem = pl.BlockSpec(memory_space=pltpu.SMEM)
    zsz = ns // (2 if ns % 2 == 0 else 1)
    dma = pltpu.SemaphoreType.DMA
    steps = max(zsz - 1, 1)
    return pl.pallas_call(
        functools.partial(kernel, ns, nh, groups, entries),
        out_shape=jax.ShapeDtypeStruct(queries.shape, jnp.bfloat16),
        in_specs=[vmem, vmem, vmem, smem, smem, vmem],
        out_specs=vmem,
        scratch_shapes=[
            pltpu.VMEM((groups, nh, rows, width), jnp.bfloat16),
            pltpu.VMEM((groups, nh, rows, width), jnp.bfloat16),
            pltpu.VMEM((entries * BLOCK_ROWS, HEAD_SIZE), jnp.bfloat16),
            pltpu.VMEM((entries * BLOCK_ROWS, 2 * HEAD_SIZE), jnp.bfloat16),
            pltpu.VMEM((2 * BLOCK_ROWS, BLOCK_ROWS), jnp.float32),
            pltpu.VMEM((ns, 1, 128), jnp.int32),
            pltpu.SMEM((ns, 1, 128), jnp.int32),
            dma((groups, 2, nh - 1)), dma((groups, 2, nh - 1)),
            dma((groups, nh - 1)), dma((groups, nh - 1)),
            dma((groups, steps)), dma((groups, steps)),
            dma((groups, steps)), dma((groups, steps)),
            dma((groups, 2 * zsz)), dma((groups, 2 * zsz)),
            dma((groups, nh - 1)), dma((groups, nh - 1)),
            dma((ns - 1,)), dma((ns - 1,)),
            dma,
        ] + [pltpu.VMEM((ns * nh, 2, BLOCK_ROWS, HEAD_SIZE), jnp.bfloat16)] * groups,
        compiler_params=pltpu.CompilerParams(
            collective_id=0, has_side_effects=True, vmem_limit_bytes=60 * 1024 * 1024),
        name="block_attention",
    )(queries, keys, values, selected, counts, slots)


def solution(mesh):
    return jax.shard_map(
        body,
        mesh=mesh,
        in_specs=(
            P(("seq", "head"), None),
            P(("seq", "head"), None),
            P(("seq", "head"), None),
            P("seq", None),
            P("seq"),
            P("seq"),
        ),
        out_specs=P(("seq", "head"), None),
        check_vma=False,
    )
```

time: 247 us -> 86.1 us (0.35)
  Pallas kernels: 0 us -> 81.6 us
  blocking collectives: 71.1 us -> 0 us
  waiting for transfers between devices: 57.7 us -> 0 us
  matrix products: 44.9 us -> 0 us
  local copies, waits for them, and re-layouts: 39 us -> 4.26 us
  starting transfers between devices: 18.3 us -> 0 us
  other arithmetic: 10.8 us -> 0 us
  loops' own time: 3.02 us -> 0 us
    pallas_call x0 -> x1, Pallas kernels: none -> 81.6 us  [body(): pl.pallas_call(functools.partial(kernel, ns, nh, groups, entries), out_sh...]
    all_to_all x2 -> x0, blocking collectives: 58 us -> none  [the longest x1 29.2 us: body(): lax.all_to_all(attended, 'head', split_axis=0, concat_axis=1, tiled=True)]
    all_to_all x5 -> x0, waiting for transfers between devices: 57.7 us -> none  [the longest x1 24.4 us: body(): lax.all_to_all(queries, 'head', split_axis=1, concat_axis=0, tiled=True)]
    sub x4 -> x0, matrix products: 27.4 us -> none  [attend(): weights = jnp.exp(scores - row_top)]
    all_to_all x5 -> x0, starting transfers between devices: 18.3 us -> none  [the longest x1 4.63 us: body(): lax.all_to_all(queries, 'head', split_axis=1, concat_axis=0, tiled=True)]
    dot_general x7 -> x0, matrix products: 17.6 us -> none  [the longest x4 16.8 us: attend(): jnp.einsum('gmik,kgd->igmd', probability, value_block_rows, preferred_ele...]
    gather x10 -> x0, local copies, waits for them, and re-layouts: 14 us -> none  [the longest x4 6.41 us: attend(): got_keys[place_row]]
    unnamed x1 -> x0, blocking collectives: 13.1 us -> none
  transfers between devices with their start and end apart: 5 -> 0, of which waited for: 5 -> 0; matrix products, arithmetic and copies ran while one was open for 5% -> 0% of each run, Pallas kernels for 0% -> 0%
where the time goes in v1:
time: 86.1 us; the launch traced here: 85.9 us
  Pallas kernels  81.6 us (95%)
  local copies, waits for them, and re-layouts  4.26 us (5%)
    pallas_call x1, Pallas kernels, body(): pl.pallas_call(functools.partial(kernel, ns, nh, groups, entries), out_sh...  81.6 us
    unnamed x1, local copies, waits for them, and re-layouts  3.1 us

profile of v1, /device:TPU:0, one launch (start us, length us, event | category | flops | bytes accessed | tf_op | source)
XLA Modules:
  0.0 85.9 jit_solution(13299375556722879214)
XLA Ops:
  0.0 1.2 %pad_bitcast_fusion.slot_ref = s32[1,128]{1,0:T(1,128)} fusion(s32[4]{0:T(128)} %param.11), kind=kLoop, calls=%fused_computation | loop fusion | bytes 528 | tf_op jit(solution)/shard_map/reshape | solution.py:283
  1.2 81.6 %block_attention.1 = bf16[128,8192]{1,0:T(8,128)(2,1)} custom-call(bf16[128,8192]{1,0:T(8,128)(2,1)} %q_ref.1, bf16[128,1024]{1,0:T(8,128)(2,1)} %k_ref.1, bf16[128,1024]{1,0:T(8,128)(2,1)} %v_ref.1, s32[4,8]{1,0:T(4,128)} %sel_ref.1, s32[4]{0:T(128)} %cnt_ref.1, s32[1,128]{1,0:T(1,128)} %pad_bitcast_fusion.slot_ref), custom_call_target="tpu_custom_call" | custom-call | tf_op jit(solution)/shard_map/block_attention/pallas_call | solution.py:289
  82.8 3.1 %copy.8 = bf16[128,8192]{1,0:T(8,128)(2,1)} copy(bf16[128,8192]{1,0:T(8,128)(2,1)} %block_attention.1) | data formatting | bytes 4194304

commit v2 on v1

--- a/solution.py
+++ b/solution.py
@@ -15,8 +15,8 @@
 MESH = pl.DeviceIdType.MESH
 
 
-def kernel(ns, nh, groups, entries, q_ref, k_ref, v_ref, sel_ref, cnt_ref, slot_ref, out_ref,
-           qbuf, obuf, kcat, vcat, diag, slots_v, slots_s,
+def kernel(ns, nh, groups, entries, q_ref, k_ref, v_ref, sel_ref, cnt_ref, own_slot_ref, out_ref,
+           qbuf, obuf, kcat, vcat, diag, slot_ref, slots_v, slots_s,
            hs, hr, qs, qr, us, ur, ds_, dr, ys, yr, os_, or_, ss, sr, slot_sem, *kv):
     s = lax.axis_index("seq")
     h = lax.axis_index("head")
@@ -34,6 +34,12 @@
             src_ref=src, dst_ref=dst, send_sem=send, recv_sem=recv,
             device_id=dev, device_id_type=MESH)
 
+    lane = lax.broadcasted_iota(jnp.int32, (1, 128), 1)
+    slot_row = jnp.zeros((1, 128), jnp.int32)
+    for i in range(sel_ref.shape[0]):
+        slot_row = jnp.where(lane == i, own_slot_ref[i], slot_row)
+    slot_ref[...] = slot_row
+
     barrier = pltpu.get_barrier_semaphore()
     for d in range(1, nh):
         pl.semaphore_signal(barrier, inc=1, device_id=(s, (h + d) % nh), device_id_type=MESH)
@@ -94,88 +100,124 @@
     diag[...] = jnp.where(col <= row, 0.0, -jnp.inf).astype(jnp.float32)
     vcat[:, HEAD_SIZE:] = jnp.ones((entries * BLOCK_ROWS, HEAD_SIZE), jnp.bfloat16)
 
-    def chunk(g, shard):
-        return kv[g].at[pl.ds(shard * nh, nh)]
-
-    def up(g, t, shard, dev):
-        return remote(chunk(g, shard), chunk(g, shard), us.at[g, t], ur.at[g, t], (dev, h))
-
-    def down(g, t, shard, dev):
-        return remote(chunk(g, shard), chunk(g, shard), ds_.at[g, t], dr.at[g, t], (dev, h))
-
-    def across(g, i, shard):
-        return remote(chunk(g, shard), chunk(g, shard), ys.at[g, i], yr.at[g, i], (y_peer, h))
-
-    def gather_start(g):
-        for d in rotation:
-            for t in range(2):
-                kv_head_in(g, t, d).wait_recv()
-        if ysz > 1:
-            across(g, 0, s).start()
+    half = nh // 2
+
+    def early(g):
+        return ysz > 1 and nh > 2 and g == groups - 1
+
+    def part(g, shard, piece):
+        lo, size = ((0, half), (half, nh - half), (nh - 1, 1))[piece]
+        return kv[g].at[pl.ds(shard * nh + lo, size)]
+
+    def cross_part(g, shard, piece):
+        if piece == 1 and early(g):
+            return kv[g].at[pl.ds(shard * nh + half, nh - 1 - half)]
+        return part(g, shard, piece)
+
+    def up(g, p, t, shard, dev):
+        ref = part(g, shard, p)
+        return remote(ref, ref, us.at[g, p, t], ur.at[g, p, t], (dev, h))
+
+    def down(g, p, t, shard, dev):
+        ref = part(g, shard, p)
+        return remote(ref, ref, ds_.at[g, p, t], dr.at[g, p, t], (dev, h))
+
+    def across(g, p, i, shard):
+        ref = cross_part(g, shard, p)
+        return remote(ref, ref, ys.at[g, p, i], yr.at[g, p, i], (y_peer, h))
+
+    def pieces(g):
+        return (0, 1, 2) if early(g) else (0, 1)
+
+    def column(p):
+        return y_peer if p == 2 else s
+
+    def send_both(g, p):
         if zsz > 1:
             @pl.when(z < zsz - 1)
             def _():
-                up(g, 0, s, s + ysz).start()
+                up(g, p, 0, column(p), s + ysz).start()
 
             @pl.when(z > 0)
             def _():
-                down(g, 0, s, s - ysz).start()
+                down(g, p, 0, column(p), s - ysz).start()
+
+    def gather_z(g):
+        for d in rotation:
+            for t in range(2):
+                kv_head_in(g, t, d).wait_recv()
+        if early(g):
+            across(g, 2, 0, s).start()
+        send_both(g, 0)
+        send_both(g, 1)
+
+    def gather_y(g):
+        if ysz > 1:
+            across(g, 0, 0, s).start()
+            across(g, 1, 0, s).start()
+        if early(g):
+            across(g, 2, 0, y_peer).wait_recv()
+            send_both(g, 2)
 
     def gather_step(g, t):
-        below = s - (1 + t) * ysz
-        above = s + (1 + t) * ysz
-
-        @pl.when(z - 1 - t >= 0)
-        def _():
-            up(g, t, below, s).wait_recv()
-            if t + 1 < zsz - 1:
-                @pl.when(z < zsz - 1)
-                def _():
-                    up(g, t + 1, below, s + ysz).start()
-            if ysz > 1:
-                across(g, 1 + t, below).start()
-
-        @pl.when(z + 1 + t <= zsz - 1)
-        def _():
-            down(g, t, above, s).wait_recv()
-            if t + 1 < zsz - 1:
-                @pl.when(z > 0)
-                def _():
-                    down(g, t + 1, above, s - ysz).start()
-            if ysz > 1:
-                across(g, zsz + t, above).start()
+        for p in pieces(g):
+            below = column(p) - (1 + t) * ysz
+            above = column(p) + (1 + t) * ysz
+
+            @pl.when(z - 1 - t >= 0)
+            def _():
+                up(g, p, t, below, s).wait_recv()
+                if t + 1 < zsz - 1:
+                    @pl.when(z < zsz - 1)
+                    def _():
+                        up(g, p, t + 1, below, s + ysz).start()
+                if ysz > 1 and p < 2:
+                    across(g, p, 1 + t, below).start()
+
+            @pl.when(z + 1 + t <= zsz - 1)
+            def _():
+                down(g, p, t, above, s).wait_recv()
+                if t + 1 < zsz - 1:
+                    @pl.when(z > 0)
+                    def _():
+                        down(g, p, t + 1, above, s - ysz).start()
+                if ysz > 1 and p < 2:
+                    across(g, p, zsz + t, above).start()
 
     def gather_end(g):
         if ysz > 1:
-            across(g, 0, y_peer).wait_recv()
+            for p in range(2):
+                across(g, p, 0, y_peer).wait_recv()
             for t in range(zsz - 1):
-                @pl.when(z - 1 - t >= 0)
+                for p in range(2):
+                    @pl.when(z - 1 - t >= 0)
+                    def _():
+                        across(g, p, 1 + t, y_peer - (1 + t) * ysz).wait_recv()
+
+                    @pl.when(z + 1 + t <= zsz - 1)
+                    def _():
+                        across(g, p, zsz + t, y_peer + (1 + t) * ysz).wait_recv()
+
+    def gather_drain(g):
+        for p in pieces(g):
+            if ysz > 1:
+                across(g, p, 0, s).wait_send()
+            for t in range(zsz - 1):
+                @pl.when((z < zsz - 1) & (z - t >= 0))
                 def _():
-                    across(g, 1 + t, y_peer - (1 + t) * ysz).wait_recv()
-
-                @pl.when(z + 1 + t <= zsz - 1)
+                    up(g, p, t, column(p) - t * ysz, s + ysz).wait_send()
+
+                @pl.when((z > 0) & (z + t <= zsz - 1))
                 def _():
-                    across(g, zsz + t, y_peer + (1 + t) * ysz).wait_recv()
-
-    def gather_drain(g):
-        if ysz > 1:
-            across(g, 0, s).wait_send()
-        for t in range(zsz - 1):
-            @pl.when((z < zsz - 1) & (z - t >= 0))
-            def _():
-                up(g, t, s - t * ysz, s + ysz).wait_send()
-
-            @pl.when((z > 0) & (z + t <= zsz - 1))
-            def _():
-                down(g, t, s + t * ysz, s - ysz).wait_send()
-            if ysz > 1:
-                @pl.when(z - 1 - t >= 0)
-                def _():
-                    across(g, 1 + t, s - (1 + t) * ysz).wait_send()
-
-                @pl.when(z + 1 + t <= zsz - 1)
-                def _():
-                    across(g, zsz + t, s + (1 + t) * ysz).wait_send()
+                    down(g, p, t, column(p) + t * ysz, s - ysz).wait_send()
+                if ysz > 1 and p < 2:
+                    @pl.when(z - 1 - t >= 0)
+                    def _():
+                        across(g, p, 1 + t, s - (1 + t) * ysz).wait_send()
+
+                    @pl.when(z + 1 + t <= zsz - 1)
+                    def _():
+                        across(g, p, zsz + t, s + (1 + t) * ysz).wait_send()
 
     factor = math.log2(math.e) / math.sqrt(HEAD_SIZE)
     blk_seq = sel_ref.shape[0]
@@ -209,7 +251,7 @@
             obuf[g, j, :, pl.ds(cols + HEAD_SIZE, HEAD_SIZE)] = result[BLOCK_ROWS:]
             return 0
 
-        lax.fori_loop(0, heads_per_group // 2, pair, 0)
+        lax.fori_loop(0, heads_per_group // 2, pair, 0, unroll=True)
 
     def result_out(g, d):
         peer = (h + d) % nh
@@ -221,38 +263,51 @@
         return remote(obuf.at[g, peer], out_ref.at[:, lanes(peer * groups + g, width)],
                       os_.at[g, d - 1], or_.at[g, d - 1], (s, peer))
 
-    gather_start(0)
-    for t in range(zsz - 1):
+    def slot_table():
+        for d in range(1, ns):
+            slot_in(d).wait_recv()
+        slot_copy = pltpu.make_async_copy(slots_v, slots_s, slot_sem)
+        slot_copy.start()
+        slot_copy.wait()
+
+    if nh == 4:
+        order = [2, 3 - 2 * (h % 2), 1 + 2 * (h % 2), 0]
+    else:
+        order = rotation + [0]
+    gather_z(0)
+    gather_y(0)
+    for t in range(zsz - 2):
         gather_step(0, t)
-    for d in range(1, ns):
-        slot_in(d).wait_recv()
-    slot_copy = pltpu.make_async_copy(slots_v, slots_s, slot_sem)
-    slot_copy.start()
-    slot_copy.wait()
-
-    order = rotation + [0]
     pending = None
     for g in range(groups):
+        more = g + 1 < groups
+        if more:
+            gather_z(g + 1)
+        if g == 0 and zsz > 1:
+            gather_step(0, zsz - 2)
         steps = []
-        if g + 1 < groups:
-            gather_start(g + 1)
+        if more:
+            gather_y(g + 1)
             steps = list(range(zsz - 1))
             if steps:
                 gather_step(g + 1, steps.pop(0))
+        if g == 0:
+            slot_table()
         gather_end(g)
-        for d in order:
+        for n, d in enumerate(order):
+            own = n == len(order) - 1
             j = (h + d) % nh
             fetch(g, j)
             if pending is not None:
                 result_out(*pending).start()
                 pending = None
-            if d:
+            if not own:
                 q_head_in(g, nh - d).wait_recv()
             attend(g, j)
-            if d:
+            if own:
+                out_ref[:, lanes(h * groups + g, width)] = obuf[g, h]
+            else:
                 pending = (g, d)
-            else:
-                out_ref[:, lanes(h * groups + g, width)] = obuf[g, h]
             if steps:
                 gather_step(g + 1, steps.pop(0))
         for t in steps:
@@ -280,7 +335,6 @@
     groups = keys.shape[1] // HEAD_SIZE // nh
     width = queries.shape[1] // nh // groups
     assert rows == BLOCK_ROWS and blk_seq == nh
-    slots = jnp.pad(block_slot, (0, 128 - blk_seq)).reshape(1, 128)
     vmem = pl.BlockSpec(memory_space=pltpu.VMEM)
     smem = pl.BlockSpec(memory_space=pltpu.SMEM)
     zsz = ns // (2 if ns % 2 == 0 else 1)
@@ -289,7 +343,7 @@
     return pl.pallas_call(
         functools.partial(kernel, ns, nh, groups, entries),
         out_shape=jax.ShapeDtypeStruct(queries.shape, jnp.bfloat16),
-        in_specs=[vmem, vmem, vmem, smem, smem, vmem],
+        in_specs=[vmem, vmem, vmem, smem, smem, smem],
         out_specs=vmem,
         scratch_shapes=[
             pltpu.VMEM((groups, nh, rows, width), jnp.bfloat16),
@@ -297,13 +351,14 @@
             pltpu.VMEM((entries * BLOCK_ROWS, HEAD_SIZE), jnp.bfloat16),
             pltpu.VMEM((entries * BLOCK_ROWS, 2 * HEAD_SIZE), jnp.bfloat16),
             pltpu.VMEM((2 * BLOCK_ROWS, BLOCK_ROWS), jnp.float32),
+            pltpu.VMEM((1, 128), jnp.int32),
             pltpu.VMEM((ns, 1, 128), jnp.int32),
             pltpu.SMEM((ns, 1, 128), jnp.int32),
             dma((groups, 2, nh - 1)), dma((groups, 2, nh - 1)),
             dma((groups, nh - 1)), dma((groups, nh - 1)),
-            dma((groups, steps)), dma((groups, steps)),
-            dma((groups, steps)), dma((groups, steps)),
-            dma((groups, 2 * zsz)), dma((groups, 2 * zsz)),
+            dma((groups, 3, steps)), dma((groups, 3, steps)),
+            dma((groups, 3, steps)), dma((groups, 3, steps)),
+            dma((groups, 3, 2 * zsz)), dma((groups, 3, 2 * zsz)),
             dma((groups, nh - 1)), dma((groups, nh - 1)),
             dma((ns - 1,)), dma((ns - 1,)),
             dma,
@@ -311,7 +366,7 @@
         compiler_params=pltpu.CompilerParams(
             collective_id=0, has_side_effects=True, vmem_limit_bytes=60 * 1024 * 1024),
         name="block_attention",
-    )(queries, keys, values, selected, counts, slots)
+    )(queries, keys, values, selected, counts, block_slot)
 
 
 def solution(mesh):

time: 86.1 us -> 80.1 us (0.930)
  Pallas kernels: 81.6 us -> 76.8 us
  local copies, waits for them, and re-layouts: 4.26 us -> 3.1 us
    pallas_call x1, Pallas kernels: 81.6 us -> 76.8 us  [body(): pl.pallas_call(functools.partial(kernel, ns, nh, groups, entries), out_sh...]
    reshape x1 -> x0, local copies, waits for them, and re-layouts: 1.17 us -> none  [body(): slots = jnp.pad(block_slot, (0, 128 - blk_seq)).reshape(1, 128)]
where the time goes in v2:
time: 80.1 us; the launch traced here: 79.9 us
  Pallas kernels  76.8 us (96%)
  local copies, waits for them, and re-layouts  3.1 us (4%)
    pallas_call x1, Pallas kernels, body(): pl.pallas_call(functools.partial(kernel, ns, nh, groups, entries), out_sh...  76.8 us
    unnamed x1, local copies, waits for them, and re-layouts  3.1 us

profile of v2, /device:TPU:0, one launch (start us, length us, event | category | flops | bytes accessed | tf_op | source)
XLA Modules:
  0.0 79.9 jit_solution(2118703923463779810)
XLA Ops:
  0.0 76.8 %block_attention.1 = bf16[128,8192]{1,0:T(8,128)(2,1)} custom-call(bf16[128,8192]{1,0:T(8,128)(2,1)} %q_ref.1, bf16[128,1024]{1,0:T(8,128)(2,1)} %k_ref.1, bf16[128,1024]{1,0:T(8,128)(2,1)} %v_ref.1, s32[4,8]{1,0:T(4,128)} %sel_ref.1, s32[4]{0:T(128)} %cnt_ref.1, s32[4]{0:T(128)} %own_slot_ref.1), custom_call_target="tpu_custom_call" | custom-call | tf_op jit(solution)/shard_map/block_attention/pallas_call | solution.py:343
  76.8 3.1 %copy.8 = bf16[128,8192]{1,0:T(8,128)(2,1)} copy(bf16[128,8192]{1,0:T(8,128)(2,1)} %block_attention.1) | data formatting | bytes 4194304

commit v3 on v2

--- a/solution.py
+++ b/solution.py
@@ -303,13 +303,13 @@
                 pending = None
             if not own:
                 q_head_in(g, nh - d).wait_recv()
+            if n >= len(order) // 2 and len(steps) > 1:
+                gather_step(g + 1, steps.pop(0))
             attend(g, j)
             if own:
                 out_ref[:, lanes(h * groups + g, width)] = obuf[g, h]
             else:
                 pending = (g, d)
-            if steps:
-                gather_step(g + 1, steps.pop(0))
         for t in steps:
             gather_step(g + 1, t)
 

time: 80.1 us -> 79.1 us (0.988)
  Pallas kernels: 76.8 us -> 75.8 us
    pallas_call x1, Pallas kernels: 76.8 us -> 75.8 us  [body(): pl.pallas_call(functools.partial(kernel, ns, nh, groups, entries), out_sh...]
where the time goes in v3:
time: 79.1 us; the launch traced here: 78.9 us
  Pallas kernels  75.8 us (96%)
  local copies, waits for them, and re-layouts  3.1 us (4%)
    pallas_call x1, Pallas kernels, body(): pl.pallas_call(functools.partial(kernel, ns, nh, groups, entries), out_sh...  75.8 us
    unnamed x1, local copies, waits for them, and re-layouts  3.1 us

profile of v3, /device:TPU:0, one launch (start us, length us, event | category | flops | bytes accessed | tf_op | source)
XLA Modules:
  0.0 78.9 jit_solution(7053085162907909545)
XLA Ops:
  0.0 75.8 %block_attention.1 = bf16[128,8192]{1,0:T(8,128)(2,1)} custom-call(bf16[128,8192]{1,0:T(8,128)(2,1)} %q_ref.1, bf16[128,1024]{1,0:T(8,128)(2,1)} %k_ref.1, bf16[128,1024]{1,0:T(8,128)(2,1)} %v_ref.1, s32[4,8]{1,0:T(4,128)} %sel_ref.1, s32[4]{0:T(128)} %cnt_ref.1, s32[4]{0:T(128)} %own_slot_ref.1), custom_call_target="tpu_custom_call" | custom-call | tf_op jit(solution)/shard_map/block_attention/pallas_call | solution.py:343
  75.8 3.1 %copy.8 = bf16[128,8192]{1,0:T(8,128)(2,1)} copy(bf16[128,8192]{1,0:T(8,128)(2,1)} %block_attention.1) | data formatting | bytes 4194304
